TPU v7x, 32 devices: a whole 2x2x4 slice. The times are simulated.
32 devices in a mesh: dp: 4 (over z), mp: 8 (over y, x, core).
Axes of the slice: x: 2, y: 2, z: 4, core: 2. Of those that a mesh axis runs over, the one named last changes fastest.
Arguments:
- grad_parts: bfloat16 [4, 8, 2, 18432, 128], P('dp', 'mp'), may hold values from -45 to 45
- master: float32 [8, 2, 18432, 128], P('mp', None, 'dp'), may hold values from -15 to 15
- momenta: float32 [3, 8, 2, 18432, 128], P(None, 'mp', None, 'dp'), may hold values from -45 to 45
- second: float32 [3, 8, 2, 18432, 128], P(None, 'mp', None, 'dp'), may hold values from 0.00025 to 330
- step_count: int32 [1], replicated, may hold values from 1 to 99999
- mlp_first: float32 [8, 4], replicated, may hold values from -2 to 2
- mlp_bias: float32 [4], replicated, may hold values from -3 to 3
- mlp_second: float32 [4, 2], replicated, may hold values from -3 to 3
- tensor_weight: float32 [10], replicated, may hold values from -2 to 2
Outputs:
- new_params: bfloat16 [8, 2, 18432, 128], P('mp')
- new_master: float32 [8, 2, 18432, 128], P('mp', None, 'dp')
- new_momenta: float32 [3, 8, 2, 18432, 128], P(None, 'mp', None, 'dp')
- new_second: float32 [3, 8, 2, 18432, 128], P(None, 'mp', None, 'dp')
- update: float32 [8, 2, 18432, 128], P('mp', None, 'dp')
All inputs are finite; a program needn't handle non-finite values.
Results may differ from a plain program's by a relative error of at most 0.019.
Values may be sent and summed in bfloat16 or wider, within the bound.
A program may use at most 192 MiB of HBM per device.

v0:
```python
import jax
import jax.numpy as jnp
from jax import lax
from jax.sharding import PartitionSpec as P

D = 4608
HQ = 4096


RATES = (0.9, 0.99, 0.999)


def advance(gradient, momenta, second):
    moments = jnp.stack(
        [rate * momenta[i] + (1.0 - rate) * gradient for i, rate in enumerate(RATES)]
    )
    squares = jnp.stack(
        [rate * second[i] + (1.0 - rate) * gradient * gradient for i, rate in enumerate(RATES)]
    )
    return (moments, squares)


def features_of(master, gradient, moments, squares):
    listing = [master, gradient, moments[0], moments[1], moments[2]]
    for slot_id in range(3):
        listing.append(moments[slot_id] / jnp.sqrt(squares[slot_id]))
    return listing


def perceptron(normed, boost, mlp_first, mlp_bias, mlp_second):
    direction = jnp.zeros_like(normed[0])
    magnitude = jnp.zeros_like(normed[0])
    for unit_id in range(mlp_first.shape[1]):
        active = mlp_first[0, unit_id] * normed[0]
        for feat_id in range(1, len(normed)):
            active = active + mlp_first[feat_id, unit_id] * normed[feat_id]
        active = jax.nn.relu(active + mlp_bias[unit_id])
        direction = direction + mlp_second[unit_id, 0] * active
        magnitude = magnitude + mlp_second[unit_id, 1] * active
    return direction * jnp.exp(0.5 * jnp.tanh(magnitude)) * boost


def tensor_boost(norms, step_count, tensor_weight):
    count = tensor_weight.shape[0] - 2
    step_value = step_count[0].astype(jnp.float32)
    first_phase = jnp.log1p(step_value) / 11.5
    second_phase = step_value / 100000.0
    logits = jnp.sum(tensor_weight[:count, None] * jnp.log(norms), axis=0)
    logits = logits + tensor_weight[count] * first_phase + tensor_weight[count + 1] * second_phase
    return jnp.exp(jnp.tanh(logits))


def square_sums(listing):
    return jnp.stack([jnp.sum(feature * feature, axis=(0, 2, 3)) for feature in listing])


def local(
    grad_parts, master, momenta, second, step_count, mlp_first, mlp_bias, mlp_second, tensor_weight
):
    gradient = lax.psum_scatter(grad_parts, "dp", scatter_dimension=3, tiled=True).astype(
        jnp.float32
    )[0]
    new_momenta, new_second = advance(gradient, momenta, second)
    early_local = square_sums([master, gradient])
    listing = features_of(master, gradient, new_momenta, new_second)
    late_local = square_sums(listing[2:])
    totals = lax.psum(jnp.concatenate([early_local, late_local], axis=0), ("dp", "mp"))
    norms = jnp.sqrt(totals / float(D * HQ) + 1e-06)
    boost = tensor_boost(norms, step_count, tensor_weight)[None, :, None, None]
    normed = [listing[i] / norms[i][None, :, None, None] for i in range(len(listing))]
    update = perceptron(normed, boost, mlp_first, mlp_bias, mlp_second)
    new_master = master - 0.05 * update
    new_params = lax.all_gather(new_master.astype(jnp.bfloat16), "dp", axis=2, tiled=True)
    return (new_params, new_master, new_momenta, new_second, update)


def solution(mesh):
    placed = (
        P("dp", "mp", None, None, None),
        P("mp", None, "dp", None),
        P(None, "mp", None, "dp", None),
        P(None, "mp", None, "dp", None),
        P(),
        P(),
        P(),
        P(),
        P(),
    )
    return jax.shard_map(
        local,
        mesh=mesh,
        in_specs=placed,
        out_specs=(
            P("mp", None, None, None),
            P("mp", None, "dp", None),
            P(None, "mp", None, "dp", None),
            P(None, "mp", None, "dp", None),
            P("mp", None, "dp", None),
        ),
        check_vma=False,
    )
```

profile of v0, /device:TPU:0, one launch (start us, length us, event | category | flops | bytes accessed | tf_op | source)
XLA Modules:
  0.0 466.4 jit_solution(5703901997524263589)
XLA Ops:
  7.2 0.0 reduce-scatter.2.cloned.1.call-start
  7.2 0.7 reduce-scatter.2.cloned.1.call-update
  7.9 0.0 copy-start.4
  7.9 0.0 copy-start.3
  7.9 0.0 copy-start.2
  7.9 0.0 copy-start.1
  7.9 0.0 all-gather.2.cloned.1.call-start
  8.7 3.0 multiply_reduce_fusion.6
  11.7 0.1 copy.22
  11.8 0.0 copy-done.4
  11.8 0.6 fusion.33
  13.1 0.0 copy-done.3
  13.1 0.6 fusion.32
  13.7 0.0 copy-done.2
  13.7 0.7 fusion.31
  14.4 0.0 copy-done.1
  14.4 0.7 fusion.30
  15.1 0.7 fusion.29
  15.9 158.4 %reduce-scatter.2.cloned.1.call-done = bf16[1,1,2,4608,128]{4,3,2,1,0:T(8,128)(2,1)} async-done(((bf16[1,1,2,18432,128]{4,3,2,1,0:T(8,128)(2,1)}), bf16[1,1,2,4608,128]{4,3,2,1,0:T(8,128)(2,1)}) %reduce-scatter.2.cloned.1.call-update) | async-done | bytes 2359312 | tf_op jit(solution)/shard_map/reduce_scatter | solution.py:60
  174.3 0.0 copy-start
  174.3 14.4 %multiply_reduce_fusion = (f32[2]{0:T(128)S(1)}, f32[2]{0:T(128)S(1)}, f32[2]{0:T(128)S(1)}, f32[2]{0:T(128)S(1)}, f32[2]{0:T(128)S(1)}, /*index=5*/f32[2]{0:T(128)S(1)}, f32[2]{0:T(128)S(1)}) fusion(bf16[1,1,2,4608,128]{4,3,2,1,0:T(8,128)(2,1)} %reduce-scatter.2.cloned.1.call-done, f32[3,1,2,4608,128]{4,3,2,1,0:T(8,128)} %param.12, ...), kind=kLoop, calls=%fused_computation.38 | loop fusion | flops 42467320 | bytes 30670904 | tf_op jit(solution)/shard_map/reduce_sum | solution.py:54
  188.7 0.1 copy.27
  188.8 0.1 copy.29
  188.9 0.1 copy.28
  189.0 0.1 copy.24
  189.1 0.1 copy.25
  189.2 0.1 copy.26
  189.2 0.1 copy.23
  189.3 0.1 concatenate.3
  190.1 41.2 %psum.7 = f32[8,2]{0,1:T(2,128)S(1)} all-reduce(f32[8,2]{0,1:T(2,128)S(1)} %concatenate.3), channel_id=1, replica_groups=mesh['dp'=4,'mp'=8] {'dp','mp'}, use_global_device_ids=true, to_apply=%region_9.0 | all-reduce | flops 16 | bytes 128 | tf_op jit(solution)/shard_map/psum | solution.py:67
  231.3 0.1 fusion.27
  231.4 0.3 slice_reduce_fusion.7
  231.7 0.0 copy-done
  231.7 52.0 %fusion.28 = (bf16[1,2,4608,128]{3,2,1,0:T(8,128)(2,1)}, f32[1,2,4608,128]{3,2,1,0:T(8,128)}, f32[1,2,4608,128]{3,2,1,0:T(8,128)}) fusion(f32[1,2,4608,128]{3,2,1,0:T(8,128)} %param.10, f32[2]{0:T(128)S(1)} %tanh_exponential_fusion, f32[]{:T(128)} %bitcast.58, f32[]{:T(128)} %bitcast.57, f32[]{:T(128)} %bitcast.56, f32[]{:T(128)} %bitcast.55, f32[]{:T(128)} %bitcast.54, ...), kind=kLoop, calls=%fused_computation.64 | loop fusion | flops 139198464 | bytes 47186168 | tf_op jit(solution)/shard_map/convert_element_type | solution.py:73
  283.7 0.0 all-gather.2.cloned.1.call-update
  283.7 20.3 %fusion.24 = (f32[1,1,2,4608,128]{4,3,2,1,0:T(8,128)}, f32[1,1,2,4608,128]{4,3,2,1,0:T(8,128)}, f32[1,1,2,4608,128]{4,3,2,1,0:T(8,128)}, f32[1,1,2,4608,128]{4,3...) fusion(bf16[1,1,2,4608,128]{4,3,2,1,0:T(8,128)(2,1)S(1)} %copy-done, ...), kind=kLoop, calls=%fused_computation.33 | loop fusion | flops 22413312 | bytes 58982400 | tf_op jit(solution)/shard_map/add | solution.py:18
  304.1 18.9 %pad_maximum_fusion = (f32[3,1,2,4608,128]{4,3,2,1,0:T(8,128)}, f32[3,1,2,4608,128]{4,3,2,1,0:T(8,128)}) fusion(f32[1,1,2,4608,128]{4,3,2,1,0:T(8,128)} %get-tuple-element.29, f32[1,1,2,4608,128]{4,3,2,1,0:T(8,128)} %get-tuple-element.30, f32[1,1,2,4608,128]{4,3,2,1,0:T(8,128)} %get-tuple-element.31, f32[1,1,2,4608,128]{4,3,2,1,0:T(8,128)} %get-tuple-element.25, ...), kind=kLoop, calls=%fused_computation | loop fusion | flops 14155776 | bytes 56623104 | tf_op jit(solution)/shard_map/stack | solution.py:14
  323.0 127.5 %all-gather.2.cloned.1.call-done = bf16[1,2,18432,128]{3,2,1,0:T(8,128)(2,1)} async-done(((bf16[1,2,4608,128]{3,2,1,0:T(8,128)(2,1)}), bf16[1,2,18432,128]{3,2,1,0:T(8,128)(2,1)}) %all-gather.2.cloned.1.call-update) | async-done | bytes 9437200 | tf_op jit(solution)/shard_map/all_gather | solution.py:73
  450.4 9.1 %copy.32 = bf16[1,2,18432,128]{3,2,1,0:T(8,128)(2,1)} copy(bf16[1,2,18432,128]{3,2,1,0:T(8,128)(2,1)} %all-gather.2.cloned.1.call-done) | data formatting | bytes 18874368
  (2 shorter events, 0.0 us)
Async XLA Ops:
  7.2 167.1 %reduce-scatter.2.cloned.1.call-start = ((), (), s32[]{:S(2)}) async-start(), calls=%async_computation.1 | async-start | bytes 11796480 | tf_op jit(solution)/shard_map/reduce_scatter | solution.py:60
  7.9 3.9 copy-start.4
  7.9 5.1 %copy-start.3 = (f32[4]{0:T(128)S(1)}, f32[4]{0:T(128)}, u32[]{:S(2)}) copy-start(f32[4]{0:T(128)} %param.15) | copy-start | bytes 52
  7.9 5.8 %copy-start.2 = (f32[4,2]{0,1:T(2,128)S(1)}, f32[4,2]{0,1:T(2,128)}, u32[]{:S(2)}) copy-start(f32[4,2]{0,1:T(2,128)} %param.16) | copy-start | bytes 100
  7.9 6.5 %copy-start.1 = (f32[8,4]{0,1:T(4,128)S(1)}, f32[8,4]{0,1:T(4,128)}, u32[]{:S(2)}) copy-start(f32[8,4]{0,1:T(4,128)} %param.14) | copy-start | bytes 388
  7.9 442.5 %all-gather.2.cloned.1.call-start = ((), (), s32[]{:S(2)}) async-start(), calls=%async_computation.2 | async-start | bytes 11796480 | tf_op jit(solution)/shard_map/all_gather | solution.py:73
  174.3 57.4 %copy-start = (bf16[1,1,2,4608,128]{4,3,2,1,0:T(8,128)(2,1)S(1)}, bf16[1,1,2,4608,128]{4,3,2,1,0:T(8,128)(2,1)}, u32[]{:S(2)}) copy-start(bf16[1,1,2,4608,128]{4,3,2,1,0:T(8,128)(2,1)} %reduce-scatter.2.cloned.1.call-done) | copy-start | bytes 7077892
Sparse Core Ops, SparseCore 0:
  10.3 163.9 reduce-scatter.1
  283.9 166.5 all-gather.1
where the time goes:
time: 467 us; the launch traced here: 466 us
  waiting for transfers between devices  287 us (61%)
  other arithmetic  109 us (23%)
  blocking collectives  41.2 us (9%)
  between operations  16.1 us (3%)
  local copies, waits for them, and re-layouts  13.6 us (3%)
    reduce_scatter x1, waiting for transfers between devices, local(): lax.psum_scatter(grad_parts, 'dp', scatter_dimension=3, tiled=True)  158 us
    all_gather x1, waiting for transfers between devices, local(): lax.all_gather(new_master.astype(jnp.bfloat16), 'dp', axis=2, tiled=True)  127 us
    convert_element_type x1, other arithmetic, local(): new_master.astype(jnp.bfloat16)  52 us
    psum x1, blocking collectives, local(): lax.psum(jnp.concatenate([early_local, late_local], axis=0), ('dp', 'mp'))  41.2 us
    add x1, other arithmetic, advance(): rate * second[i] + (1.0 - rate) * gradient * gradient  20.3 us
    another operation x1, other arithmetic, advance(): jnp.stack([rate * momenta[i] + (1.0 - rate) * gradient for i, rate in enu...  18.9 us
    reduce_sum x2, other arithmetic, square_sums(): jnp.sum(feature * feature, axis=(0, 2, 3))  17.4 us
  transfers between devices with their start and end apart: 2, of which 2 were waited for; matrix products, arithmetic and copies ran while one was open for 10% of the time, Pallas kernels for 0%

commit v1 on v0

v1 whole, which is shorter than its diff:
```python
import functools

import jax
import jax.numpy as jnp
from jax import lax
from jax.experimental import pallas as pl
from jax.experimental.pallas import tpu as pltpu
from jax.sharding import PartitionSpec as P

D = 4608
HQ = 4096
RATES = (0.9, 0.99, 0.999)
MESH = pl.DeviceIdType.MESH
STRIP = 32


def block_rows(rows, most=1152):
    best = STRIP
    for size in range(STRIP, most + 1, STRIP):
        if rows % size == 0:
            best = size
    return best


def advanced(g, momenta, second):
    moments = [b * m + (1.0 - b) * g for b, m in zip(RATES, momenta)]
    gg = g * g
    squares = [b * s + (1.0 - b) * gg for b, s in zip(RATES, second)]
    return moments, squares


def listing_of(master, g, moments, squares):
    ratios = [m * lax.rsqrt(s) for m, s in zip(moments, squares)]
    return [master, g, *moments, *ratios]


def update_of(listing, coef, base, feats, hidden):
    direction = None
    magnitude = None
    tail = base + feats * hidden
    for j in range(hidden):
        active = listing[0] * coef[base + j] + coef[tail + j]
        for f in range(1, feats):
            active = active + listing[f] * coef[base + f * hidden + j]
        active = jnp.maximum(active, 0.0)
        d = active * coef[tail + hidden + j]
        m = active * coef[tail + 2 * hidden + j]
        direction = d if direction is None else direction + d
        magnitude = m if magnitude is None else magnitude + m
    return direction * jnp.exp(0.5 * jnp.tanh(magnitude))


def stats_kernel(steps, g_ref, master_ref, mom_ref, sec_ref, *rest):
    out_ref, acc = rest[-2:]
    i = pl.program_id(0)

    @pl.when(i == 0)
    def _():
        acc[...] = jnp.zeros_like(acc)

    def body(k, carry):
        rows = pl.ds(pl.multiple_of(k * STRIP, STRIP), STRIP)
        g = g_ref[rows, :].astype(jnp.float32)
        moments, squares = advanced(
            g, [mom_ref[c, 0, 0, rows, :] for c in range(3)], [sec_ref[c, 0, 0, rows, :] for c in range(3)]
        )
        feats = listing_of(master_ref[0, 0, rows, :], g, moments, squares)
        return tuple(
            a + jnp.sum((f * f).reshape(STRIP // 8, 8, 128), axis=0) for a, f in zip(carry, feats)
        )

    sums = lax.fori_loop(0, g_ref.shape[0] // STRIP, body, tuple(acc[f] for f in range(8)))
    for f in range(8):
        acc[f] = sums[f]

    @pl.when(i == steps - 1)
    def _():
        for f in range(8):
            out_ref[pl.ds(f, 1), :] = jnp.sum(acc[f], axis=0, keepdims=True)


def state_specs(rows, t_of):
    return [
        pl.BlockSpec((1, 1, rows, 128), lambda *a: (0, t_of(a), a[-1], 0)),
        pl.BlockSpec((3, 1, 1, rows, 128), lambda *a: (0, 0, t_of(a), a[-1], 0)),
        pl.BlockSpec((3, 1, 1, rows, 128), lambda *a: (0, 0, t_of(a), a[-1], 0)),
    ]


def cost(elements, flops, nbytes):
    return pl.CostEstimate(flops=elements * flops, bytes_accessed=nbytes, transcendentals=5 * elements)


def stats(t, g, master, momenta, second, after=()):
    own = g.shape[0]
    rows = block_rows(own)
    steps = own // rows
    return pl.pallas_call(
        functools.partial(stats_kernel, steps),
        grid=(steps,),
        out_shape=jax.ShapeDtypeStruct((8, 128), jnp.float32),
        in_specs=[pl.BlockSpec((rows, 128), lambda i: (i, 0))] + state_specs(rows, lambda a: t)
        + [pl.BlockSpec(memory_space=pl.ANY)] * len(after),
        out_specs=pl.BlockSpec((8, 128), lambda i: (0, 0)),
        scratch_shapes=[pltpu.VMEM((8, 8, 128), jnp.float32)],
        cost_estimate=cost(own * 128, 40, own * 128 * 30),
        name=f"stats{t}",
    )(g, master, momenta, second, *after)


def params_kernel(feats, hidden, coef, g_ref, master_ref, mom_ref, sec_ref, out_ref):
    def body(k, carry):
        rows = pl.ds(pl.multiple_of(k * STRIP, STRIP), STRIP)
        g = g_ref[rows, :].astype(jnp.float32)
        moments, squares = advanced(
            g, [mom_ref[c, 0, 0, rows, :] for c in range(3)], [sec_ref[c, 0, 0, rows, :] for c in range(3)]
        )
        master = master_ref[0, 0, rows, :]
        update = update_of(listing_of(master, g, moments, squares), coef, 0, feats, hidden)
        out_ref[rows, :] = (master - 0.05 * update).astype(jnp.bfloat16)
        return carry

    lax.fori_loop(0, g_ref.shape[0] // STRIP, body, 0)


def params(t, feats, hidden, coef, g, master, momenta, second):
    own = g.shape[0]
    rows = block_rows(own)
    return pl.pallas_call(
        functools.partial(params_kernel, feats, hidden),
        grid=(own // rows,),
        out_shape=jax.ShapeDtypeStruct((own, 128), jnp.bfloat16),
        in_specs=[pl.BlockSpec(memory_space=pltpu.SMEM), pl.BlockSpec((rows, 128), lambda i: (i, 0))]
        + state_specs(rows, lambda a: t),
        out_specs=pl.BlockSpec((rows, 128), lambda i: (i, 0)),
        cost_estimate=cost(own * 128, 130, own * 128 * 32),
        name=f"params{t}",
    )(coef, g, master, momenta, second)


def finish_kernel(
    feats, hidden, width, coef, g0_ref, g1_ref, master_ref, mom_ref, sec_ref, nm_ref, nmom_ref, nsec_ref, up_ref
):
    t = pl.program_id(0)
    base = t * width

    def body(k, carry):
        rows = pl.ds(pl.multiple_of(k * STRIP, STRIP), STRIP)
        g = jnp.where(t == 0, g0_ref[rows, :].astype(jnp.float32), g1_ref[rows, :].astype(jnp.float32))
        moments, squares = advanced(
            g, [mom_ref[c, 0, 0, rows, :] for c in range(3)], [sec_ref[c, 0, 0, rows, :] for c in range(3)]
        )
        for c in range(3):
            nmom_ref[c, 0, 0, rows, :] = moments[c]
            nsec_ref[c, 0, 0, rows, :] = squares[c]
        master = master_ref[0, 0, rows, :]
        update = update_of(listing_of(master, g, moments, squares), coef, base, feats, hidden)
        up_ref[0, 0, rows, :] = update
        nm_ref[0, 0, rows, :] = master - 0.05 * update
        return carry

    lax.fori_loop(0, g0_ref.shape[0] // STRIP, body, 0)


def finish(feats, hidden, coefs, g0, g1, master, momenta, second):
    own = g0.shape[0]
    rows = block_rows(own)
    steps = own // rows
    width = coefs.shape[0] // 2
    specs = state_specs(rows, lambda a: a[0])
    return pl.pallas_call(
        functools.partial(finish_kernel, feats, hidden, width),
        grid=(2, steps),
        out_shape=(
            jax.ShapeDtypeStruct(master.shape, jnp.float32),
            jax.ShapeDtypeStruct(momenta.shape, jnp.float32),
            jax.ShapeDtypeStruct(second.shape, jnp.float32),
            jax.ShapeDtypeStruct(master.shape, jnp.float32),
        ),
        in_specs=[
            pl.BlockSpec(memory_space=pltpu.SMEM),
            pl.BlockSpec((rows, 128), lambda t, i: (i * (1 - t) + (steps - 1) * t, 0)),
            pl.BlockSpec((rows, 128), lambda t, i: (i * t, 0)),
        ]
        + specs,
        out_specs=(specs[0], specs[1], specs[2], specs[0]),
        cost_estimate=cost(2 * own * 128, 130, 2 * own * 128 * 62),
        name="finish",
    )(coefs, g0, g1, master, momenta, second)


def total_kernel(n_dp, n_mp, x_ref, out_ref, near, far, send1, recv1, send2, recv2, local_sem):
    z = lax.axis_index("dp")
    m = lax.axis_index("mp")
    mine = pltpu.make_async_copy(x_ref, near.at[0], local_sem)
    mine.start()
    barrier = pltpu.get_barrier_semaphore()
    for j in range(1, n_mp):
        pl.semaphore_signal(barrier, inc=1, device_id=(z, lax.rem(m + j, n_mp)), device_id_type=MESH)
    for j in range(1, n_dp):
        pl.semaphore_signal(barrier, inc=1, device_id=(lax.rem(z + j, n_dp), m), device_id_type=MESH)
    pl.semaphore_wait(barrier, n_mp - 1 + n_dp - 1)
    first = []
    for j in range(1, n_mp):
        copy = pltpu.make_async_remote_copy(
            src_ref=x_ref,
            dst_ref=near.at[j],
            send_sem=send1.at[j],
            recv_sem=recv1.at[j],
            device_id=(z, lax.rem(m + j, n_mp)),
            device_id_type=MESH,
        )
        copy.start()
        first.append(copy)
    mine.wait()
    for copy in first:
        copy.wait()
    second = []
    for j in range(1, n_dp):
        copy = pltpu.make_async_remote_copy(
            src_ref=near,
            dst_ref=far.at[j - 1],
            send_sem=send2.at[j],
            recv_sem=recv2.at[j],
            device_id=(lax.rem(z + j, n_dp), m),
            device_id_type=MESH,
        )
        copy.start()
        second.append(copy)
    for copy in second:
        copy.wait()
    total = jnp.sum(near[...], axis=0)
    for j in range(n_dp - 1):
        total = total + jnp.sum(far[j], axis=0)
    out_ref[...] = total


def total(which, n_dp, n_mp, x):
    return pl.pallas_call(
        functools.partial(total_kernel, n_dp, n_mp),
        out_shape=jax.ShapeDtypeStruct(x.shape, x.dtype),
        in_specs=[pl.BlockSpec(memory_space=pltpu.VMEM)],
        out_specs=pl.BlockSpec(memory_space=pltpu.VMEM),
        scratch_shapes=[
            pltpu.VMEM((n_mp,) + x.shape, x.dtype),
            pltpu.VMEM((n_dp - 1, n_mp) + x.shape, x.dtype),
            pltpu.SemaphoreType.DMA((n_mp,)),
            pltpu.SemaphoreType.DMA((n_mp,)),
            pltpu.SemaphoreType.DMA((n_dp,)),
            pltpu.SemaphoreType.DMA((n_dp,)),
            pltpu.SemaphoreType.DMA,
        ],
        compiler_params=pltpu.CompilerParams(collective_id=which, has_side_effects=True),
        cost_estimate=pl.CostEstimate(flops=1000, bytes_accessed=10_000_000, transcendentals=0),
        name=f"total{which}",
    )(x)


def coef_kernel(totals_ref, step_ref, first_ref, bias_ref, second_ref, weight_ref, out_ref):
    feats, hidden = first_ref.shape
    sums = jnp.sum(totals_ref[...], axis=1, keepdims=True) + jnp.zeros((feats, 128), jnp.float32)
    norms = jnp.sqrt(sums / float(D * HQ) + 1e-06)
    logs = jnp.log(norms)
    inverse = 1.0 / norms
    step = jnp.full((1, 128), step_ref[0].astype(jnp.float32))
    logits = weight_ref[feats] * (jnp.log(1.0 + step) / 11.5) + weight_ref[feats + 1] * (step / 100000.0)
    for f in range(feats):
        logits = logits + weight_ref[f] * logs[f : f + 1, :]
    boost = jnp.exp(jnp.tanh(logits))[0, 0]
    for f in range(feats):
        scale = inverse[f, 0]
        for j in range(hidden):
            out_ref[f * hidden + j] = first_ref[f, j] * scale
    tail = feats * hidden
    for j in range(hidden):
        out_ref[tail + j] = bias_ref[j]
        out_ref[tail + hidden + j] = second_ref[j, 0] * boost
        out_ref[tail + 2 * hidden + j] = second_ref[j, 1]


def coefficients(totals, step_count, mlp_first, mlp_bias, mlp_second, tensor_weight):
    feats, hidden = mlp_first.shape
    smem = pl.BlockSpec(memory_space=pltpu.SMEM)
    return pl.pallas_call(
        coef_kernel,
        out_shape=jax.ShapeDtypeStruct(((feats + 3) * hidden,), jnp.float32),
        in_specs=[pl.BlockSpec(memory_space=pltpu.VMEM)] + [smem] * 5,
        out_specs=smem,
        name="coefficients",
    )(totals, step_count, mlp_first, mlp_bias, mlp_second, tensor_weight)


def pick_kernel(x_ref, out_ref):
    out_ref[...] = x_ref[0, 0, 0]


def pick(t, grad_parts):
    total_rows = grad_parts.shape[3]
    rows = block_rows(total_rows, 4608)
    return pl.pallas_call(
        pick_kernel,
        grid=(total_rows // rows,),
        out_shape=jax.ShapeDtypeStruct(grad_parts.shape[3:], grad_parts.dtype),
        in_specs=[pl.BlockSpec((1, 1, 1, rows, 128), lambda i: (0, 0, t, i, 0))],
        out_specs=pl.BlockSpec((rows, 128), lambda i: (i, 0)),
        cost_estimate=pl.CostEstimate(flops=0, bytes_accessed=4 * total_rows * 128, transcendentals=0),
        name=f"pick{t}",
    )(grad_parts)


def local(
    n_dp, n_mp, grad_parts, master, momenta, second, step_count, mlp_first, mlp_bias, mlp_second, tensor_weight
):
    feats, hidden = mlp_first.shape
    net = (step_count, mlp_first, mlp_bias, mlp_second, tensor_weight)
    g0 = lax.psum_scatter(pick(0, grad_parts), "dp", scatter_dimension=0, tiled=True)
    g0, part1 = lax.optimization_barrier((g0, pick(1, grad_parts)))
    g1 = lax.psum_scatter(part1, "dp", scatter_dimension=0, tiled=True)
    coef0 = coefficients(total(0, n_dp, n_mp, stats(0, g0, master, momenta, second)), *net)
    p0 = params(0, feats, hidden, coef0, g0, master, momenta, second)
    full0 = lax.all_gather(p0, "dp", axis=0, tiled=True)
    coef1 = coefficients(total(1, n_dp, n_mp, stats(1, g1, master, momenta, second, (p0,))), *net)
    p1 = params(1, feats, hidden, coef1, g1, master, momenta, second)
    full1 = lax.all_gather(p1, "dp", axis=0, tiled=True)
    new_master, new_momenta, new_second, update = finish(
        feats, hidden, jnp.concatenate([coef0, coef1]), g0, g1, master, momenta, second
    )
    out = jnp.stack([full0, full1])[None]
    return (out, new_master, new_momenta, new_second, update)


def solution(mesh):
    placed = (
        P("dp", "mp", None, None, None),
        P("mp", None, "dp", None),
        P(None, "mp", None, "dp", None),
        P(None, "mp", None, "dp", None),
        P(),
        P(),
        P(),
        P(),
        P(),
    )
    return jax.shard_map(
        functools.partial(local, mesh.shape["dp"], mesh.shape["mp"]),
        mesh=mesh,
        in_specs=placed,
        out_specs=(
            P("mp", None, None, None),
            P("mp", None, "dp", None),
            P(None, "mp", None, "dp", None),
            P(None, "mp", None, "dp", None),
            P("mp", None, "dp", None),
        ),
        check_vma=False,
    )
```

time: 467 us -> 391 us (0.84)
  Pallas kernels: 0 us -> 127 us
  other arithmetic: 109 us -> 9.76 us
  waiting for transfers between devices: 287 us -> 239 us
  blocking collectives: 41.2 us -> 0 us
  local copies, waits for them, and re-layouts: 13.6 us -> 1.36 us
    pallas_call x0 -> x11, Pallas kernels: none -> 127 us  [the longest x1 33.8 us: finish(): pl.pallas_call(functools.partial(finish_kernel, feats, hidden, width), gr...]
    convert_element_type x1 -> x0, other arithmetic: 52 us -> none  [local(): new_master.astype(jnp.bfloat16)]
    psum x1 -> x0, blocking collectives: 41.2 us -> none  [local(): lax.psum(jnp.concatenate([early_local, late_local], axis=0), ('dp', 'mp'))]
    reduce_scatter x1 -> x2, waiting for transfers between devices: 158 us -> 130 us  [the longest x1 83.1 us: local(): lax.psum_scatter(pick(0, grad_parts), 'dp', scatter_dimension=0, tiled=True)]
    add x1 -> x0, other arithmetic: 20.3 us -> none  [advance(): rate * second[i] + (1.0 - rate) * gradient * gradient]
    another operation x1 -> x0, other arithmetic: 18.9 us -> none  [advance(): jnp.stack([rate * momenta[i] + (1.0 - rate) * gradient for i, rate in enu...]
    all_gather x1 -> x2, waiting for transfers between devices: 127 us -> 109 us  [the longest x1 89.1 us: local(): full1 = lax.all_gather(p1, 'dp', axis=0, tiled=True)]
    reduce_sum x2 -> x0, other arithmetic: 17.4 us -> none  [square_sums(): jnp.sum(feature * feature, axis=(0, 2, 3))]
  transfers between devices with their start and end apart: 2 -> 4, of which waited for: 2 -> 4; matrix products, arithmetic and copies ran while one was open for 10% -> 1% of each run, Pallas kernels for 0% -> 31%
where the time goes in v1:
time: 391 us
  waiting for transfers between devices  239 us (61%)
  Pallas kernels  127 us (32%)
  between operations  14.5 us (4%)
  other arithmetic  9.76 us (2%)
    all_gather x1, waiting for transfers between devices, local(): full1 = lax.all_gather(p1, 'dp', axis=0, tiled=True)  89.1 us
    reduce_scatter x1, waiting for transfers between devices, local(): lax.psum_scatter(pick(0, grad_parts), 'dp', scatter_dimension=0, tiled=True)  83.1 us
    reduce_scatter x1, waiting for transfers between devices, local(): g1 = lax.psum_scatter(part1, 'dp', scatter_dimension=0, tiled=True)  46.6 us
    pallas_call x1, Pallas kernels, finish(): pl.pallas_call(functools.partial(finish_kernel, feats, hidden, width), gr...  33.8 us
    pallas_call x2, Pallas kernels, params(): pl.pallas_call(functools.partial(params_kernel, feats, hidden), grid=(own...  31.8 us
    pallas_call x2, Pallas kernels, total(): pl.pallas_call(functools.partial(total_kernel, n_dp, n_mp), out_shape=jax...  29.8 us
    all_gather x1, waiting for transfers between devices, local(): full0 = lax.all_gather(p0, 'dp', axis=0, tiled=True)  19.6 us
    pallas_call x2, Pallas kernels, stats(): pl.pallas_call(functools.partial(stats_kernel, steps), grid=(steps,), out...  17.8 us
  transfers between devices with their start and end apart: 4, of which 4 were waited for; matrix products, arithmetic and copies ran while one was open for 1% of the time, Pallas kernels for 31%

profile of v1, /device:TPU:0, one launch (start us, length us, event | category | flops | bytes accessed | tf_op | source)
XLA Modules:
  0.0 390.9 jit_solution(6471757492708821159)
XLA Ops:
  7.2 0.0 reduce-scatter.3.cloned.1.call-start
  7.2 5.0 %pick0.1 = bf16[18432,128]{1,0:T(8,128)(2,1)} custom-call(bf16[1,1,2,18432,128]{4,3,2,1,0:T(8,128)(2,1)} %x_ref.3), custom_call_target="tpu_custom_call" | custom-call | bytes 9437184 | tf_op jit(solution)/shard_map/pick0/pallas_call | solution.py:300
  12.2 0.0 reduce-scatter.3.cloned.1.call-update
  12.3 0.0 reduce-scatter.5.cloned.1.call-start
  12.3 5.0 %pick1.1 = bf16[18432,128]{1,0:T(8,128)(2,1)} custom-call(bf16[1,1,2,18432,128]{4,3,2,1,0:T(8,128)(2,1)} %x_ref.3), custom_call_target="tpu_custom_call" | custom-call | bytes 9437184 | tf_op jit(solution)/shard_map/pick1/pallas_call | solution.py:300
  17.4 0.0 copy-start.3
  17.4 83.1 %reduce-scatter.3.cloned.1.call-done.g_ref.g0_ref = bf16[4608,128]{1,0:T(8,128)(2,1)} async-done(((bf16[18432,128]{1,0:T(8,128)(2,1)}), bf16[4608,128]{1,0:T(8,128)(2,1)}) %reduce-scatter.3.cloned.1.call-update) | async-done | bytes 1179664 | tf_op jit(solution)/shard_map/reduce_scatter | solution.py:316
  100.4 0.0 reduce-scatter.5.cloned.1.call-update
  100.5 0.0 all-gather.3.cloned.1.call-start
  101.2 0.0 copy-done.3
  101.2 0.7 copy.15.second_ref
  101.8 0.0 copy-start.2
  101.8 8.9 %stats0.1.x_ref = f32[8,128]{1,0:T(8,128)} custom-call(bf16[4608,128]{1,0:T(8,128)(2,1)} %reduce-scatter.3.cloned.1.call-done.g_ref.g0_ref, f32[1,2,4608,128]{3,2,1,0:T(8,128)} %master_ref.9, f32[3,1,2,4608,128]{4,3,2,1,0:T(8,128)} %mom_ref.9, f32[3,1,2,4608,128]{4,3,2,1,0:T(8,128)} %sec_ref.9), custom_call_target="tpu_custom_call" | custom-call | flops 23592960 | bytes 17694720 | tf_op jit(solution)/shard_map/stats0/pallas_call | solution.py:98
  110.8 0.0 copy-done.2
  110.8 0.7 copy.14.first_ref
  111.4 15.6 %total0.1.totals_ref = f32[8,128]{1,0:T(8,128)} custom-call(f32[8,128]{1,0:T(8,128)} %stats0.1.x_ref), custom_call_target="tpu_custom_call" | custom-call | flops 1000 | bytes 10000000 | tf_op jit(solution)/shard_map/total0/pallas_call | solution.py:239
  127.0 1.6 coefficients.2.coef
  128.6 15.9 %params0.1.rest_0_ = bf16[4608,128]{1,0:T(8,128)(2,1)} custom-call(f32[44]{0:T(128)} %coefficients.2.coef, bf16[4608,128]{1,0:T(8,128)(2,1)} %reduce-scatter.3.cloned.1.call-done.g_ref.g0_ref, f32[1,2,4608,128]{3,2,1,0:T(8,128)} %master_ref.9, f32[3,1,2,4608,128]{4,3,2,1,0:T(8,128)} %mom_ref.9, f32[3,1,2,4608,128]{4,3,2,1,0:T(8,128)} %sec_ref.9), custom_call_target="tpu_custom_call" | custom-call | flops 76677120 | bytes 18874368 | tf_op jit(solution)/shard_map/params0/pallas_call | solution.py:129
  144.5 0.0 all-gather.3.cloned.1.call-update
  144.6 0.0 all-gather.5.cloned.1.call-start
  144.6 46.6 %reduce-scatter.5.cloned.1.call-done.g_ref.g1_ref = bf16[4608,128]{1,0:T(8,128)(2,1)} async-done(((bf16[18432,128]{1,0:T(8,128)(2,1)}), bf16[4608,128]{1,0:T(8,128)(2,1)}) %reduce-scatter.5.cloned.1.call-update) | async-done | bytes 1179664 | tf_op jit(solution)/shard_map/reduce_scatter | solution.py:318
  191.3 8.9 %stats1.1.x_ref = f32[8,128]{1,0:T(8,128)} custom-call(bf16[4608,128]{1,0:T(8,128)(2,1)} %reduce-scatter.5.cloned.1.call-done.g_ref.g1_ref, f32[1,2,4608,128]{3,2,1,0:T(8,128)} %master_ref.9, f32[3,1,2,4608,128]{4,3,2,1,0:T(8,128)} %mom_ref.9, f32[3,1,2,4608,128]{4,3,2,1,0:T(8,128)} %sec_ref.9, bf16[4608,128]{1,0:T(8,128)(2,1)} %params0.1.rest_0_), custom_call_target="tpu_custom_call" | custom-call | flops 23592960 | bytes 17694720 | tf_op jit(solution)/shard_map/stats1/pallas_call | solution.py:98
  200.2 14.3 %total1.1.totals_ref = f32[8,128]{1,0:T(8,128)} custom-call(f32[8,128]{1,0:T(8,128)} %stats1.1.x_ref), custom_call_target="tpu_custom_call" | custom-call | flops 1000 | bytes 10000000 | tf_op jit(solution)/shard_map/total1/pallas_call | solution.py:239
  214.5 1.6 coefficients.3.coef
  216.1 0.0 copy-start
  216.1 0.0 copy-start.1
  216.1 15.9 %params1.1 = bf16[4608,128]{1,0:T(8,128)(2,1)} custom-call(f32[44]{0:T(128)} %coefficients.3.coef, bf16[4608,128]{1,0:T(8,128)(2,1)} %reduce-scatter.5.cloned.1.call-done.g_ref.g1_ref, f32[1,2,4608,128]{3,2,1,0:T(8,128)} %master_ref.9, f32[3,1,2,4608,128]{4,3,2,1,0:T(8,128)} %mom_ref.9, f32[3,1,2,4608,128]{4,3,2,1,0:T(8,128)} %sec_ref.9), custom_call_target="tpu_custom_call" | custom-call | flops 76677120 | bytes 18874368 | tf_op jit(solution)/shard_map/params1/pallas_call | solution.py:129
  232.0 0.0 all-gather.5.cloned.1.call-update
  232.0 0.0 copy-done
  232.0 0.0 copy-done.1
  232.1 0.7 pad_maximum_fusion.coef
  232.7 33.8 %finish.1 = (f32[1,2,4608,128]{3,2,1,0:T(8,128)}, f32[3,1,2,4608,128]{4,3,2,1,0:T(8,128)}, f32[3,1,2,4608,128]{4,3,2,1,0:T(8,128)}, f32[1,2,4608,128]{3,2,1,0:T(8,128)}) custom-call(f32[88]{0:T(128)} %pad_maximum_fusion.coef, bf16[4608,128]{1,0:T(8,128)(2,1)} %reduce-scatter.3.cloned.1.call-done.g_ref.g0_ref, ...), custom_call_target="tpu_custom_call" | custom-call | flops 153354240 | bytes 73138176 | tf_op jit(solution)/shard_map/finish/pallas_call | solution.py:171
  266.5 19.6 %all-gather.3.cloned.1.call-done = bf16[18432,128]{1,0:T(8,128)(2,1)} async-done(((bf16[4608,128]{1,0:T(8,128)(2,1)}), bf16[18432,128]{1,0:T(8,128)(2,1)}) %all-gather.3.cloned.1.call-update) | async-done | bytes 4718608 | tf_op jit(solution)/shard_map/all_gather | solution.py:321
  286.2 89.1 %all-gather.5.cloned.1.call-done = bf16[18432,128]{1,0:T(8,128)(2,1)} async-done(((bf16[4608,128]{1,0:T(8,128)(2,1)}), bf16[18432,128]{1,0:T(8,128)(2,1)}) %all-gather.5.cloned.1.call-update) | async-done | bytes 4718608 | tf_op jit(solution)/shard_map/all_gather | solution.py:324
  375.2 9.1 %maximum_bitcast_fusion = bf16[1,2,18432,128]{3,2,1,0:T(8,128)(2,1)} fusion(bf16[1,18432,128]{2,1,0:T(8,128)(2,1)} %bitcast.5, bf16[1,18432,128]{2,1,0:T(8,128)(2,1)} %bitcast.4), kind=kLoop, calls=%fused_computation | loop fusion | flops 4718592 | bytes 18874368 | tf_op jit(solution)/shard_map/broadcast_in_dim | solution.py:328
Async XLA Ops:
  7.2 93.3 %reduce-scatter.3.cloned.1.call-start = ((), (), s32[]{:S(2)}) async-start(), calls=%async_computation.2 | async-start | bytes 5898240 | tf_op jit(solution)/shard_map/reduce_scatter | solution.py:316
  12.3 179.0 %reduce-scatter.5.cloned.1.call-start = ((), (), s32[]{:S(2)}) async-start(), calls=%async_computation.4 | async-start | bytes 5898240 | tf_op jit(solution)/shard_map/reduce_scatter | solution.py:318
  17.4 83.8 %copy-start.3 = (f32[4,2]{0,1:T(2,128)S(1)}, f32[4,2]{0,1:T(2,128)}, u32[]{:S(2)}) copy-start(f32[4,2]{0,1:T(2,128)} %param.16) | copy-start | bytes 100
  100.5 185.7 %all-gather.3.cloned.1.call-start = ((), (), s32[]{:S(2)}) async-start(), calls=%async_computation.3 | async-start | bytes 5898240 | tf_op jit(solution)/shard_map/all_gather | solution.py:321
  101.8 8.9 %copy-start.2 = (f32[8,4]{0,1:T(4,128)S(1)}, f32[8,4]{0,1:T(4,128)}, u32[]{:S(2)}) copy-start(f32[8,4]{0,1:T(4,128)} %param.14) | copy-start | bytes 388
  144.6 230.7 %all-gather.5.cloned.1.call-start = ((), (), s32[]{:S(2)}) async-start(), calls=%async_computation.5 | async-start | bytes 5898240 | tf_op jit(solution)/shard_map/all_gather | solution.py:324
  216.1 16.0 %copy-start = (f32[44]{0:T(128)S(1)}, f32[44]{0:T(128)}, u32[]{:S(2)}) copy-start(f32[44]{0:T(128)} %coefficients.2.coef) | copy-start | bytes 532
  216.1 16.0 %copy-start.1 = (f32[44]{0:T(128)S(1)}, f32[44]{0:T(128)}, u32[]{:S(2)}) copy-start(f32[44]{0:T(128)} %coefficients.3.coef) | copy-start | bytes 532
Sparse Core Ops, SparseCore 0:
  12.4 88.0 reduce-scatter.2
  103.3 87.8 reduce-scatter.4
  193.4 92.6 all-gather.2
  287.6 87.6 all-gather.4
